TPU v7x, 32 devices: a 4x4x1 block of a 4x4x8 slice. The times are simulated.
32 devices in a mesh: dp: 1 (over z), fsdp: 32 (over y, x, core).
Axes of the slice: x: 4, y: 4, z: 1, core: 2. Of those that a mesh axis runs over, the one named last changes fastest.
The devices are a block of a 4x4x8 slice.
Arguments:
- latents: bfloat16 [2048, 16, 1152], P(('dp', 'fsdp'))
- cond_emb: bfloat16 [2048, 1152], P(('dp', 'fsdp'))
- w_ada: bfloat16 [2, 1152, 6912], P(None, 'fsdp')
- b_ada: bfloat16 [2, 6912], replicated
- w_qkv: bfloat16 [2, 1152, 3456], P(None, 'fsdp')
- b_qkv: bfloat16 [2, 3456], replicated
- w_proj: bfloat16 [2, 1152, 1152], P(None, 'fsdp')
- b_proj: bfloat16 [2, 1152], replicated
- w_fc1: bfloat16 [2, 1152, 4608], P(None, 'fsdp')
- b_fc1: bfloat16 [2, 4608], replicated
- w_fc2: bfloat16 [2, 4608, 1152], P(None, 'fsdp')
- b_fc2: bfloat16 [2, 1152], replicated
Outputs:
- output: bfloat16 [2048, 16, 1152], P(('dp', 'fsdp'))
All inputs are finite; a program needn't handle non-finite values.
Results may differ from a plain program's by a relative error of at most 0.0162659.
Values are sent between devices in bfloat16 or wider.
A program may use at most 768 MiB of HBM per device.

v0:
```python
import jax
import jax.numpy as jnp
from jax import lax
from jax.sharding import PartitionSpec as P

NUM_HEADS = 16
LN_EPS = 1e-6


def layer_norm(values_in):
    mean_val = jnp.mean(values_in, axis=-1, keepdims=True)
    centered = values_in - mean_val
    var_val = jnp.mean(centered * centered, axis=-1, keepdims=True)
    return centered * lax.rsqrt(var_val + LN_EPS)


def gather_rows(shard):
    return lax.all_gather(shard, 'fsdp', axis=0, tiled=True)


def value_a9(residual, modulation, w_qkv, b_qkv, w_proj, b_proj, w_fc1, b_fc1, w_fc2, b_fc2):
    samples, tokens, hidden = residual.shape
    head_dim = hidden // NUM_HEADS
    mod_parts = modulation.reshape(samples, 6, 1, hidden)
    shift_a = mod_parts[:, 0]
    scale_a = mod_parts[:, 1]
    gate_a = mod_parts[:, 2]
    shift_m = mod_parts[:, 3]
    scale_m = mod_parts[:, 4]
    gate_m = mod_parts[:, 5]
    resid_a = residual.astype(jnp.float32)
    normed = (layer_norm(resid_a) * (1.0 + scale_a) + shift_a).astype(jnp.bfloat16)
    full_qkv = gather_rows(w_qkv)
    qkv_rows = (jnp.einsum('toe,ef->tof', normed, full_qkv, preferred_element_type=jnp.float32) + b_qkv.astype(jnp.float32)).astype(jnp.bfloat16)
    qkv_rows = qkv_rows.reshape(samples, tokens, 3, NUM_HEADS, head_dim)
    scores = jnp.einsum('sqhd,skhd->shqk', qkv_rows[:, :, 0], qkv_rows[:, :, 1], preferred_element_type=jnp.float32) * (head_dim ** -0.5)
    attn_probs = jax.nn.softmax(scores, axis=-1).astype(jnp.bfloat16)
    attn_out = jnp.einsum('shqk,skhd->sqhd', attn_probs, qkv_rows[:, :, 2], preferred_element_type=jnp.float32).astype(jnp.bfloat16).reshape(samples, tokens, hidden)
    full_proj = gather_rows(w_proj)
    proj_out = jnp.einsum('toe,ef->tof', attn_out, full_proj, preferred_element_type=jnp.float32) + b_proj.astype(jnp.float32)
    resid_b = (resid_a + gate_a * proj_out).astype(jnp.bfloat16).astype(jnp.float32)
    normed_b = (layer_norm(resid_b) * (1.0 + scale_m) + shift_m).astype(jnp.bfloat16)
    full_fc1 = gather_rows(w_fc1)
    pre_act = jnp.einsum('toe,ef->tof', normed_b, full_fc1, preferred_element_type=jnp.float32) + b_fc1.astype(jnp.float32)
    hidden_act = jax.nn.gelu(pre_act, approximate=True).astype(jnp.bfloat16)
    full_fc2 = gather_rows(w_fc2)
    mlp_out = jnp.einsum('snf,fd->snd', hidden_act, full_fc2, preferred_element_type=jnp.float32) + b_fc2.astype(jnp.float32)
    return (resid_b + gate_m * mlp_out).astype(jnp.bfloat16)


def solution(mesh):
    batch_spec = P(('dp', 'fsdp'), None, None)
    cond_spec = P(('dp', 'fsdp'), None)
    shard_spec = P(None, 'fsdp', None)
    bias_spec = P(None, None)

    def local_run(latents, cond_emb, w_ada, b_ada, w_qkv, b_qkv, w_proj, b_proj, w_fc1, b_fc1, w_fc2, b_fc2):
        cond_act = jax.nn.silu(cond_emb.astype(jnp.float32)).astype(jnp.bfloat16)
        residual = latents
        for layer_idx in range(w_ada.shape[0]):
            full_ada = gather_rows(w_ada[layer_idx])
            modulation = jnp.dot(cond_act, full_ada, preferred_element_type=jnp.float32) + b_ada[layer_idx].astype(jnp.float32)
            modulation = modulation.astype(jnp.bfloat16).astype(jnp.float32)
            residual = value_a9(residual, modulation, w_qkv[layer_idx], b_qkv[layer_idx], w_proj[layer_idx], b_proj[layer_idx], w_fc1[layer_idx], b_fc1[layer_idx], w_fc2[layer_idx], b_fc2[layer_idx])
        return residual

    in_specs = (batch_spec, cond_spec, shard_spec, bias_spec, shard_spec, bias_spec, shard_spec, bias_spec, shard_spec, bias_spec, shard_spec, bias_spec)
    return jax.shard_map(local_run, mesh=mesh, in_specs=in_specs, out_specs=batch_spec, check_vma=False)
```

profile of v0, /device:TPU:97, one launch (start us, length us, event | category | flops | bytes accessed | tf_op | source)
XLA Modules:
  0.0 758.0 jit_solution(2602385109269989632)
XLA Ops:
  6.6 4.0 fusion.178
  25.0 93.8 %all-gather.21.cloned.1.call-done = bf16[1,1152,6912]{2,0,1:T(2,128)(2,1)} async-done(((bf16[1,36,6912]{2,0,1:T(2,128)(2,1)}), bf16[1,1152,6912]{2,0,1:T(2,128)(2,1)}) %all-gather.21.cloned.1.call-update) | async-done | bytes 15925264 | tf_op jit(solution)/shard_map/all_gather | solution.py:18
  118.8 14.0 %fusion.67 = f32[64,6912]{1,0:T(8,128)} fusion(bf16[1,1152,6912]{2,0,1:T(2,128)(2,1)} %all-gather.21.cloned.1.call-done, f32[6912]{0:T(1024)S(1)} %get-tuple-element.6, bf16[64,1152]{1,0:T(8,128)(2,1)S(1)} %copy-done.19), kind=kOutput, calls=%fused_computation.57 | convolution fusion | flops 1020985344 | bytes 17869824 | tf_op jit(solution)/shard_map/dot_general | solution.py:62
  132.8 3.1 reshape.186
  135.9 8.9 %fusion.177 = (f32[64,1,1,1152]{3,1,0,2:T(1,128)S(1)}, f32[64,1,1,1152]{3,1,0,2:T(1,128)S(1)}, f32[64,1,1,1152]{3,1,0,2:T(1,128)}, f32[64,1,1,1152]{3,1,0,2:T(1,...) fusion(f32[64,6,1,1152]{3,1,0,2:T(8,128)} %reshape.186), kind=kLoop, calls=%fused_computation.195 | loop fusion | flops 147456 | bytes 3538944 | tf_op jit(solution)/shard_map/slice | solution.py:30
  145.7 39.6 %all-gather.23.cloned.1.call-done = bf16[1,1152,3456]{2,0,1:T(2,128)(2,1)} async-done(((bf16[1,36,3456]{2,0,1:T(2,128)(2,1)}), bf16[1,1152,3456]{2,0,1:T(2,128)(2,1)}) %all-gather.23.cloned.1.call-update) | async-done | bytes 7962640 | tf_op jit(solution)/shard_map/all_gather | solution.py:18
  185.4 17.8 %add_convert_fusion.1 = bf16[64,16,3456]{2,1,0:T(8,128)(2,1)} fusion(bf16[1,1152,3456]{2,0,1:T(2,128)(2,1)} %all-gather.23.cloned.1.call-done, f32[3456]{0:T(1024)S(1)} %get-tuple-element.10, bf16[64,16,1152]{2,1,0:T(8,128)(2,1)S(1)} %copy-done, f32[64,1152]{1,0:T(8,128)} %get-tuple-element.55, f32[64,1152]{1,0:T(8,128)} %get-tuple-element.56, ...), kind=kOutput, calls=%fused_computation.27 | convolution fusion | flops 8167882752 | bytes 18011648 | tf_op jit(solution)/shard_map/toe,ef->tof/dot_general | solution.py:34
  203.2 25.5 %reshape.178 = bf16[64,16,3,16,72]{4,3,2,1,0:T(8,128)(2,1)} reshape(bf16[64,16,3456]{2,1,0:T(8,128)(2,1)} %add_convert_fusion.1) | data formatting | bytes 14155776 | tf_op jit(solution)/shard_map/reshape | solution.py:35
  228.7 7.5 fusion.175
  238.5 33.3 %fusion.183 = (f32[64,16,16]{2,1,0:T(8,128)}, f32[64,16,16,16]{2,3,1,0:T(8,128)S(1)}) fusion(f32[64,16,16,16]{2,3,1,0:T(8,128)S(1)} %fusion.119), kind=kOutput, calls=%fused_computation.201 | output fusion | flops 1048591 | bytes 2162688 | tf_op jit(solution)/shard_map/sub | solution.py:37
  271.8 3.9 convert_bitcast_fusion.1
  275.7 3.1 copy.59
  278.9 7.9 %reshape.179 = bf16[64,16,1152]{2,1,0:T(8,128)(2,1)} reshape(bf16[64,16,16,72]{3,2,1,0:T(8,128)(2,1)} %copy.59) | data formatting | bytes 4718592 | tf_op jit(solution)/shard_map/reshape | solution.py:38
  287.5 3.3 all-gather.31.cloned.1.call-done
  290.8 14.2 %fusion.61 = f32[64,6912]{1,0:T(8,128)} fusion(bf16[1,1152,6912]{2,0,1:T(2,128)(2,1)} %all-gather.31.cloned.1.call-done, f32[6912]{0:T(1024)S(1)} %get-tuple-element.5, bf16[64,1152]{1,0:T(8,128)(2,1)} %param.13), kind=kOutput, calls=%fused_computation.55 | convolution fusion | flops 1020985344 | bytes 17869824 | tf_op jit(solution)/shard_map/dot_general | solution.py:62
  307.9 26.4 %all-gather.25.cloned.1.call-done = bf16[1,1152,1152]{2,0,1:T(2,128)(2,1)} async-done(((bf16[1,36,1152]{2,0,1:T(2,128)(2,1)}), bf16[1,1152,1152]{2,0,1:T(2,128)(2,1)}) %all-gather.25.cloned.1.call-update) | async-done | bytes 2654224 | tf_op jit(solution)/shard_map/all_gather | solution.py:18
  334.3 6.9 convert_reduce_fusion.2
  343.5 69.8 %all-gather.27.cloned.1.call-done = bf16[1,1152,4608]{2,0,1:T(2,128)(2,1)} async-done(((bf16[1,36,4608]{2,0,1:T(2,128)(2,1)}), bf16[1,1152,4608]{2,0,1:T(2,128)(2,1)}) %all-gather.27.cloned.1.call-update) | async-done | bytes 10616848 | tf_op jit(solution)/shard_map/all_gather | solution.py:18
  413.3 24.2 %fusion.9.clone.3.clone.4 = bf16[64,16,4608]{2,1,0:T(8,128)(2,1)} fusion(bf16[1,1152,4608]{2,0,1:T(2,128)(2,1)} %all-gather.27.cloned.1.call-done, f32[4608]{0:T(1024)S(1)} %get-tuple-element.8, bf16[64,16,1152]{2,1,0:T(8,128)(2,1)} %copy-done.5, f32[64,1152]{1,0:T(8,128)S(1)} %get-tuple-element.53, ...), kind=kOutput, calls=%fused_computation.11.clone.clone.clone.clone.clone.clone.clone.1 | convolution fusion | flops 10925899776 | bytes 23029760 | tf_op jit(solution)/shard_map/toe,ef->tof/dot_general | solution.py:44
  437.5 29.7 %all-gather.29.cloned.1.call-done = bf16[1,4608,1152]{2,1,0:T(8,128)(2,1)} async-done(((bf16[1,144,1152]{2,1,0:T(8,128)(2,1)}), bf16[1,4608,1152]{2,1,0:T(8,128)(2,1)}) %all-gather.29.cloned.1.call-update) | async-done | bytes 10616848 | tf_op jit(solution)/shard_map/all_gather | solution.py:18
  467.2 18.7 %convert_reduce_fusion.1 = (f32[64,16]{1,0:T(8,128)S(1)}, bf16[64,16,1152]{2,1,0:T(8,128)(2,1)S(1)}) fusion(f32[1152]{0:T(1024)S(1)} %get-tuple-element.12, bf16[1,4608,1152]{2,1,0:T(8,128)(2,1)} %all-gather.29.cloned.1.call-done, bf16[64,16,1152]{2,1,0:T(8,128)(2,1)} %copy-done.5, f32[64,1152]{1,0:T(8,128)S(1)} %bitcast.133, ...), kind=kOutput, calls=%fused_computation.71 | convolution fusion | flops 10879892480 | bytes 25076224 | tf_op jit(solution)/shard_map/snf,fd->snd/dot_general | solution.py:47
  489.6 44.4 %all-gather.33.cloned.1.call-done = bf16[1,1152,3456]{2,0,1:T(2,128)(2,1)} async-done(((bf16[1,36,3456]{2,0,1:T(2,128)(2,1)}), bf16[1,1152,3456]{2,0,1:T(2,128)(2,1)}) %all-gather.33.cloned.1.call-update) | async-done | bytes 7962640 | tf_op jit(solution)/shard_map/all_gather | solution.py:18
  534.0 17.8 %add_convert_fusion = bf16[64,16,3456]{2,1,0:T(8,128)(2,1)} fusion(bf16[1,1152,3456]{2,0,1:T(2,128)(2,1)} %all-gather.33.cloned.1.call-done, f32[3456]{0:T(1024)S(1)} %get-tuple-element.9, bf16[64,16,1152]{2,1,0:T(8,128)(2,1)S(1)} %get-tuple-element.48, f32[64,1152]{1,0:T(8,128)} %get-tuple-element.59, f32[64,1152]{1,0:T(8,128)} %get-tuple-element.60, ...), kind=kOutput, calls=%fused_computation.26 | convolution fusion | flops 8167882752 | bytes 18011648 | tf_op jit(solution)/shard_map/toe,ef->tof/dot_general | solution.py:34
  551.8 25.5 %reshape.182 = bf16[64,16,3,16,72]{4,3,2,1,0:T(8,128)(2,1)} reshape(bf16[64,16,3456]{2,1,0:T(8,128)(2,1)} %add_convert_fusion) | data formatting | bytes 14155776 | tf_op jit(solution)/shard_map/reshape | solution.py:35
  577.3 7.5 fusion.174
  587.1 33.3 %fusion.188 = (f32[64,16,16]{2,1,0:T(8,128)}, f32[64,16,16,16]{2,3,1,0:T(8,128)S(1)}) fusion(f32[64,16,16,16]{2,3,1,0:T(8,128)S(1)} %fusion.118), kind=kOutput, calls=%fused_computation.202 | output fusion | flops 1048591 | bytes 2162688 | tf_op jit(solution)/shard_map/sub | solution.py:37
  620.4 3.9 convert_bitcast_fusion
  627.4 6.8 reshape.183
  635.0 6.9 convert_reduce_fusion
  644.2 12.8 %all-gather.37.cloned.1.call-done = bf16[1,1152,4608]{2,0,1:T(2,128)(2,1)} async-done(((bf16[1,36,4608]{2,0,1:T(2,128)(2,1)}), bf16[1,1152,4608]{2,0,1:T(2,128)(2,1)}) %all-gather.37.cloned.1.call-update) | async-done | bytes 10616848 | tf_op jit(solution)/shard_map/all_gather | solution.py:18
  657.0 54.0 %all-gather.39.cloned.1.call-done = bf16[1,4608,1152]{2,1,0:T(8,128)(2,1)} async-done(((bf16[1,144,1152]{2,1,0:T(8,128)(2,1)}), bf16[1,4608,1152]{2,1,0:T(8,128)(2,1)}) %all-gather.39.cloned.1.call-update) | async-done | bytes 10616848 | tf_op jit(solution)/shard_map/all_gather | solution.py:18
  710.9 39.8 %fusion.107 = bf16[64,16,1152]{2,1,0:T(8,128)(2,1)} fusion(bf16[64,16,1152]{2,1,0:T(8,128)(2,1)} %copy-done.6, bf16[1,4608,1152]{2,1,0:T(8,128)(2,1)} %all-gather.39.cloned.1.call-done, bf16[1,1152,4608]{2,0,1:T(2,128)(2,1)} %all-gather.37.cloned.1.call-done, f32[4608]{0:T(1024)S(1)} %copy-done.14, f32[1152]{0:T(1024)S(1)} %copy-done.17, ...), kind=kOutput, calls=%fused_computation.105 | convolution fusion | flops 21803433984 | bytes 26868224 | tf_op jit(solution)/shard_map/snf,fd->snd/dot_general | solution.py:47
  (96 shorter events, 35.4 us)
Async XLA Ops:
  6.5 4.1 copy-start.7
  6.5 6.8 copy-start.10
  6.6 7.8 %copy-start.3 = (bf16[2,36,4608]{2,0,1:T(2,128)(2,1)S(1)}, bf16[2,36,4608]{2,0,1:T(2,128)(2,1)}, u32[]{:S(2)}) copy-start(bf16[2,36,4608]{2,0,1:T(2,128)(2,1)} %param.20) | copy-start | bytes 1990660
  6.6 112.3 %all-gather.21.cloned.1.call-start = ((), (), s32[]{:S(2)}) async-start(), calls=%async_computation | async-start | bytes 32845824 | tf_op jit(solution)/shard_map/all_gather | solution.py:18
  10.6 174.8 %all-gather.23.cloned.1.call-start = ((), (), s32[]{:S(2)}) async-start(), calls=%async_computation.1 | async-start | bytes 16422912 | tf_op jit(solution)/shard_map/all_gather | solution.py:18
  12.4 9.3 %copy-start.11 = (bf16[2,6912]{1,0:T(2,128)(2,1)S(1)}, bf16[2,6912]{1,0:T(2,128)(2,1)}, u32[]{:S(2)}) copy-start(bf16[2,6912]{1,0:T(2,128)(2,1)} %param.15) | copy-start | bytes 82948
  12.4 9.5 %copy-start = (bf16[64,16,1152]{2,1,0:T(8,128)(2,1)S(1)}, bf16[64,16,1152]{2,1,0:T(8,128)(2,1)}, u32[]{:S(2)}) copy-start(bf16[64,16,1152]{2,1,0:T(8,128)(2,1)} %param.12) | copy-start | bytes 7077892
  12.4 278.4 %all-gather.31.cloned.1.call-start = ((), (), s32[]{:S(2)}) async-start(), calls=%async_computation.5 | async-start | bytes 32845824 | tf_op jit(solution)/shard_map/all_gather | solution.py:18
  13.2 321.1 %all-gather.25.cloned.1.call-start = ((), (), s32[]{:S(2)}) async-start(), calls=%async_computation.2 | async-start | bytes 5474304 | tf_op jit(solution)/shard_map/all_gather | solution.py:18
  14.3 398.9 %all-gather.27.cloned.1.call-start = ((), (), s32[]{:S(2)}) async-start(), calls=%async_computation.3 | async-start | bytes 21897216 | tf_op jit(solution)/shard_map/all_gather | solution.py:18
  16.4 6.6 copy-start.13
  16.4 6.7 copy-start.15
  16.4 7.3 copy-start.12
  16.4 8.0 %copy-start.16 = (bf16[2,1152]{1,0:T(2,128)(2,1)S(1)}, bf16[2,1152]{1,0:T(2,128)(2,1)}, u32[]{:S(2)}) copy-start(bf16[2,1152]{1,0:T(2,128)(2,1)} %param.23) | copy-start | bytes 13828
  16.5 102.4 %copy-start.19 = (bf16[64,1152]{1,0:T(8,128)(2,1)S(1)}, bf16[64,1152]{1,0:T(8,128)(2,1)}, u32[]{:S(2)}) copy-start(bf16[64,1152]{1,0:T(8,128)(2,1)} %param.13) | copy-start | bytes 442372
  16.5 450.7 %all-gather.29.cloned.1.call-start = ((), (), s32[]{:S(2)}) async-start(), calls=%async_computation.4 | async-start | bytes 10948608 | tf_op jit(solution)/shard_map/all_gather | solution.py:18
  18.6 515.4 %all-gather.33.cloned.1.call-start = ((), (), s32[]{:S(2)}) async-start(), calls=%async_computation.6 | async-start | bytes 16422912 | tf_op jit(solution)/shard_map/all_gather | solution.py:18
  19.4 615.5 %all-gather.35.cloned.1.call-start = ((), (), s32[]{:S(2)}) async-start(), calls=%async_computation.7 | async-start | bytes 5474304 | tf_op jit(solution)/shard_map/all_gather | solution.py:18
  20.3 636.7 %all-gather.37.cloned.1.call-start = ((), (), s32[]{:S(2)}) async-start(), calls=%async_computation.8 | async-start | bytes 21897216 | tf_op jit(solution)/shard_map/all_gather | solution.py:18
  21.1 689.9 %all-gather.39.cloned.1.call-start = ((), (), s32[]{:S(2)}) async-start(), calls=%async_computation.9 | async-start | bytes 10948608 | tf_op jit(solution)/shard_map/all_gather | solution.py:18
  290.8 43.5 %copy-start.1 = (bf16[64,16,1152]{2,1,0:T(8,128)(2,1)S(1)}, bf16[64,16,1152]{2,1,0:T(8,128)(2,1)}, u32[]{:S(2)}) copy-start(bf16[64,16,1152]{2,1,0:T(8,128)(2,1)} %param.12) | copy-start | bytes 7077892
  334.3 9.1 %copy-start.8 = (f32[64,1,1,1152]{3,1,0,2:T(1,128)S(1)}, f32[64,1,1,1152]{3,1,0,2:T(1,128)}, u32[]{:S(2)}) copy-start(f32[64,1,1,1152]{3,1,0,2:T(1,128)} %get-tuple-element.29) | copy-start | bytes 884740
  341.2 1.4 copy-start.5
  467.2 19.5 %copy-start.2 = (f32[64,6,1,1152]{3,1,0,2:T(8,128)S(1)}, f32[64,6,1,1152]{3,1,0,2:T(8,128)}, u32[]{:S(2)}) copy-start(f32[64,6,1,1152]{3,1,0,2:T(8,128)} %reshape.193) | copy-start | bytes 5308420
  485.9 65.9 %copy-start.4 = (bf16[64,16,1152]{2,1,0:T(8,128)(2,1)}, bf16[64,16,1152]{2,1,0:T(8,128)(2,1)S(1)}, u32[]{:S(2)}) copy-start(bf16[64,16,1152]{2,1,0:T(8,128)(2,1)S(1)} %get-tuple-element.48) | copy-start | bytes 7077892
  627.4 7.6 %copy-start.18 = (f32[1152]{0:T(1024)S(1)}, f32[1152]{0:T(1024)}, u32[]{:S(2)}) copy-start(f32[1152]{0:T(1024)} %get-tuple-element.13) | copy-start | bytes 13828
  635.0 9.2 %copy-start.9 = (f32[64,1,1,1152]{3,1,0,2:T(1,128)S(1)}, f32[64,1,1,1152]{3,1,0,2:T(1,128)}, u32[]{:S(2)}) copy-start(f32[64,1,1,1152]{3,1,0,2:T(1,128)} %get-tuple-element.23) | copy-start | bytes 884740
  635.0 76.0 %copy-start.14 = (f32[4608]{0:T(1024)S(1)}, f32[4608]{0:T(1024)}, u32[]{:S(2)}) copy-start(f32[4608]{0:T(1024)} %get-tuple-element.7) | copy-start | bytes 55300
  635.0 75.9 %copy-start.17 = (f32[1152]{0:T(1024)S(1)}, f32[1152]{0:T(1024)}, u32[]{:S(2)}) copy-start(f32[1152]{0:T(1024)} %get-tuple-element.11) | copy-start | bytes 13828
  641.9 1.4 copy-start.6
Sparse Core Ops, SparseCore 0:
  10.7 108.0 all-gather.20
  120.9 64.4 all-gather.22
  187.5 103.2 all-gather.30
  292.8 41.4 all-gather.24
  336.3 76.9 all-gather.26
  415.3 51.9 all-gather.28
  469.3 64.6 all-gather.32
  536.1 41.6 all-gather.34
  579.9 76.9 all-gather.36
  659.0 51.9 all-gather.38
where the time goes:
time: 765 us; the launch traced here: 758 us
  waiting for transfers between devices  377 us (49%)
  matrix products  173 us (23%)
  local copies, waits for them, and re-layouts  110 us (14%)
  other arithmetic  83.2 us (11%)
  between operations  14.3 us (2%)
    all_gather x10, waiting for transfers between devices, gather_rows(): return lax.all_gather(shard, 'fsdp', axis=0, tiled=True)  374 us
    sub x2, other arithmetic, value_a9(): attn_probs = jax.nn.softmax(scores, axis=-1).astype(jnp.bfloat16)  66.6 us
    dot_general x2, matrix products, value_a9(): jnp.einsum('snf,fd->snd', hidden_act, full_fc2, preferred_element_type=jn...  58.5 us
    reshape x2, local copies, waits for them, and re-layouts, value_a9(): qkv_rows = qkv_rows.reshape(samples, tokens, 3, NUM_HEADS, head_dim)  51 us
    dot_general x2, matrix products, value_a9(): jnp.einsum('toe,ef->tof', normed, full_qkv, preferred_element_type=jnp.fl...  35.6 us
    dot_general x2, matrix products, local_run(): jnp.dot(cond_act, full_ada, preferred_element_type=jnp.float32)  28.2 us
    dot_general x1, matrix products, value_a9(): jnp.einsum('toe,ef->tof', normed_b, full_fc1, preferred_element_type=jnp....  24.2 us
  transfers between devices with their start and end apart: 10, of which 9 were waited for; matrix products, arithmetic and copies ran while one was open for 42% of the time, Pallas kernels for 0%

commit v1 on v0

v1 whole, which is shorter than its diff:
```python
import functools
import math

import jax
import jax.numpy as jnp
from jax import lax
from jax.experimental import pallas as pl
from jax.experimental.pallas import tpu as pltpu
from jax.sharding import PartitionSpec as P

NUM_HEADS = 16
LN_EPS = 1e-6
MESH = pl.DeviceIdType.MESH
BF16 = jnp.bfloat16
F32 = jnp.float32


class Gather:
    COLS = (0, -1, 1, 2)

    def __init__(self, side, dst, unit_rows, kinds, send, recv, dsend, drecv, lsem):
        self.side, self.dst, self.unit, self.kinds = side, dst, unit_rows, kinds
        self.send, self.recv, self.dsend, self.drecv, self.lsem = send, recv, dsend, drecv, lsem
        me = lax.axis_index("fsdp")
        self.core = me % 2
        self.x = (me // 2) % side
        self.y = me // (2 * side)
        self.rows = unit_rows // (side * side)

    def chip(self, core, f, g):
        x = (self.x + f * (1 - core) + g * core + self.side) % self.side
        y = (self.y + f * core + g * (1 - core) + self.side) % self.side
        return y * self.side + x

    def dev(self, f, g):
        return {"fsdp": self.chip(self.core, f, g) * 2 + self.core}

    def partner(self):
        return {"fsdp": self.chip(self.core, 0, 0) * 2 + 1 - self.core}

    def piece(self, k, core, f, g):
        pairs, first, last = self.kinds
        chip = self.chip(core, f, g)
        layer, kk = k // pairs, k % pairs
        own_order = kk // first - kk // last
        count = last - first
        plain = (2 * kk + core) * self.unit + chip * self.rows
        ordered = 2 * first * self.unit + ((chip * 2 + core) * count + kk - first) * self.rows
        row = layer * (2 * pairs * self.unit) + (1 - own_order) * plain + own_order * ordered
        return self.dst.at[pl.ds(pl.multiple_of(row, 8), self.rows), :]

    def offsets(self, tag):
        if tag == 15:
            return 0, 0
        if tag < 3:
            return (-1, 1, 2)[tag], 0
        r, w = divmod(tag - 3, 3)
        return self.COLS[r], (-1, 1, 2)[w]

    def barrier(self):
        sem = pltpu.get_barrier_semaphore()
        peers = [self.dev(1, 0), self.dev(-1, 0), self.dev(0, 1), self.dev(0, -1), self.partner()]
        for p in peers:
            pl.semaphore_signal(sem, inc=1, device_id=p, device_id_type=MESH)
        pl.semaphore_wait(sem, len(peers))

    def copy(self, k, tag, src, f, g, to):
        return pltpu.make_async_remote_copy(
            src_ref=src, dst_ref=self.piece(k, self.core, f, g), send_sem=self.send.at[k, tag],
            recv_sem=self.recv.at[k, tag], device_id=to, device_id_type=MESH)

    def dcopy(self, k, tag, src, f, g, core=None):
        return pltpu.make_async_remote_copy(
            src_ref=src, dst_ref=self.piece(k, self.core if core is None else core, f, g),
            send_sem=self.dsend.at[k, tag], recv_sem=self.drecv.at[k, tag], device_id=self.partner(),
            device_id_type=MESH)

    def got(self, k, tag):
        f, g = self.offsets(tag)
        p = self.piece(k, self.core, f, g)
        self.copy(k, tag, p, f, g, self.partner()).wait_recv()
        self.dcopy(k, tag, p, f, g).start()
        return p

    def spread2(self, k, r, src):
        f = self.COLS[r]
        self.copy(k, 3 + 3 * r, src, f, 0, self.dev(0, 1)).start()
        self.copy(k, 4 + 3 * r, src, f, 0, self.dev(0, -1)).start()

    def ring2(self, k, r):
        d = 1 - 2 * ((k + r) % 2)
        self.got(k, 3 + 3 * r)
        self.got(k, 4 + 3 * r)
        f = self.COLS[r]
        self.copy(k, 5 + 3 * r, self.piece(k, self.core, f, -d), f, -d, self.dev(0, d)).start()

    def e0(self, k, own):
        self.copy(k, 0, own, 0, 0, self.dev(1, 0)).start()
        self.copy(k, 1, own, 0, 0, self.dev(-1, 0)).start()
        self.spread2(k, 0, own)
        self.dcopy(k, 15, own, 0, 0).start()
        pltpu.make_async_copy(own, self.piece(k, self.core, 0, 0), self.lsem.at[k]).start()

    def e1(self, k):
        d = 1 - 2 * (k % 2)
        p0 = self.got(k, 0)
        p1 = self.got(k, 1)
        self.copy(k, 2, self.piece(k, self.core, -d, 0), -d, 0, self.dev(d, 0)).start()
        self.spread2(k, 1, p0)
        self.spread2(k, 2, p1)

    def e2(self, k):
        self.ring2(k, 0)
        self.spread2(k, 3, self.got(k, 2))

    def e3(self, k):
        self.ring2(k, 1)
        self.ring2(k, 2)
        self.got(k, 5)

    def e4(self, k):
        self.ring2(k, 3)
        self.got(k, 8)
        self.got(k, 11)

    def e5(self, k):
        self.got(k, 14)

    def e6(self, k):
        for tag in range(16):
            f, g = self.offsets(tag)
            p = self.piece(k, 1 - self.core, f, g)
            q = self.piece(k, self.core, f, g)
            self.dcopy(k, tag, p, f, g, 1 - self.core).wait_recv()
            self.dcopy(k, tag, q, f, g).wait_send()
            if tag < 15:
                self.copy(k, tag, q, f, g, self.partner()).wait_send()
        own = self.piece(k, self.core, 0, 0)
        pltpu.make_async_copy(own, own, self.lsem.at[k]).wait()


def normed(v):
    c = v - jnp.mean(v, axis=-1, keepdims=True)
    return c * lax.rsqrt(jnp.mean(c * c, axis=-1, keepdims=True) + LN_EPS)


def blocks_kernel(side, layers, tokens, cond_ref, x_ref, bias_ref, ada_ref, qkvw_ref, proj_ref, fc1_ref, fc2_ref, out_ref,
                  gw, act, mods, u, qkv, h, acc, wslot, f2, mask, s_ref, wsem, f2sem, *sems):
    rows, hidden = out_ref.shape
    heads, dim = NUM_HEADS, hidden // NUM_HEADS
    hk = heads * tokens
    pairs, first, last = 9, 5, 7
    n = layers * pairs
    gat = Gather(side, gw, hidden, (pairs, first, last), *sems)
    core, piece_rows = gat.core, gat.rows

    gat.barrier()

    def start_pair(k):
        layer, kk = k // pairs, k % pairs

        def send(cond, ref, col, row=0):
            @pl.when(cond)
            def _():
                own = ref.at[layer, pl.ds(pl.multiple_of(row, 8), piece_rows),
                             pl.ds(pl.multiple_of(col * hidden, 128), hidden)]
                gat.e0(k, own)

        send(kk < 3, ada_ref, 2 * kk + core)
        send(kk == 3, qkvw_ref, core)
        send(jnp.logical_and(kk == 4, core == 0), qkvw_ref, 2)
        send(jnp.logical_and(kk == 4, core == 1), proj_ref, 0)
        send(jnp.logical_and(kk >= 5, kk < 7), fc2_ref, 0, (kk - 5) * piece_rows)
        send(kk >= 7, fc1_ref, 2 * (kk - 7) + core)

    def load_pair(c):
        return pltpu.make_async_copy(gw.at[pl.ds(pl.multiple_of(2 * c * hidden, 8), 2 * hidden), :],
                                     wslot.at[(c % pairs) % 3], wsem.at[(c % pairs) % 3])

    def load_f2(c):
        row = (c // pairs) * (2 * pairs * hidden) + 2 * first * hidden
        return pltpu.make_async_copy(gw.at[pl.ds(pl.multiple_of(row, 8), 4 * hidden), :], f2, f2sem.at[0])

    def fill_mask():
        lane = lax.broadcasted_iota(jnp.int32, (hk, hidden), 1)
        row = lax.broadcasted_iota(jnp.int32, (hk, hidden), 0)
        lo = (row // tokens) * dim
        mask[...] = jnp.where(jnp.logical_and(lane >= lo, lane < lo + dim), 1.0, 0.0).astype(BF16)

    def loop(size, step, fn, unroll=1):
        def it(i, carry):
            fn(pl.multiple_of(i * step, step))
            return carry
        lax.fori_loop(0, size // step, it, 0, unroll=unroll)

    def wide(j, r, size):
        v = mods[j, pl.ds(pl.multiple_of(r // tokens, 8), size // tokens), :]
        return jnp.broadcast_to(v[:, None, :], (size // tokens, tokens, hidden)).reshape(size, hidden)

    def weight(kk, half):
        return wslot[kk % 3, half * hidden:(half + 1) * hidden, :]

    def bias(l, i):
        return bias_ref[l, i:i + 1, :]

    def modulation(l, kk):
        for half in (0, 1):
            j = 2 * kk + half
            d = jnp.dot(act[...], weight(kk, half), preferred_element_type=F32)
            mods[j] = (d + bias(l, j)).astype(BF16).astype(F32)

    LB, MB = 128, 256

    def norm_to_u(shift, scale):
        def fn(r):
            v = normed(out_ref[pl.ds(r, LB), :].astype(F32))
            u[pl.ds(r, LB), :] = (v * (1.0 + wide(scale, r, LB)) + wide(shift, r, LB)).astype(BF16)
        loop(rows, LB, fn)

    def project(l, j, kk, half):
        def fn(r):
            d = jnp.dot(u[pl.ds(r, MB), :], weight(kk, half), preferred_element_type=F32)
            qkv[j, pl.ds(r, MB), :] = (d + bias(l, 6 + j)).astype(BF16)
        loop(rows, MB, fn)

    def expand(kv):
        return jnp.broadcast_to(kv[None], (heads, tokens, hidden)).reshape(hk, hidden) * mask[...]

    def scores(half):
        def fn(r):
            r = r + half * (rows // 2)
            q = qkv[0, pl.ds(r, tokens), :]
            k = qkv[1, pl.ds(r, tokens), :]
            s_ref[pl.ds(r, tokens), :] = lax.dot_general(q, expand(k), (((1,), (1,)), ((), ())),
                                                         preferred_element_type=F32)
        loop(rows // 2, tokens, fn, unroll=4)

    def softmax():
        blk = 64

        def segment(v, op, lane_id):
            for sh in (8, 4, 2, 1):
                up, down = pltpu.roll(v, hk - sh, 1), pltpu.roll(v, sh, 1)
                v = op(v, jnp.where((lane_id // sh) % 2 == 0, up, down))
            return v

        def fn(r):
            lane_id = lax.broadcasted_iota(jnp.int32, (blk, hk), 1)
            s = s_ref[pl.ds(r, blk), :] * (dim ** -0.5)
            e = jnp.exp(s - segment(s, jnp.maximum, lane_id))
            s_ref[pl.ds(r, blk), :] = e / segment(e, jnp.add, lane_id)
        loop(rows, blk, fn)

    def values(half):
        def fn(r):
            r = r + half * (rows // 2)
            v = qkv[2, pl.ds(r, tokens), :]
            p = s_ref[pl.ds(r, tokens), :].astype(BF16)
            u[pl.ds(r, tokens), :] = jnp.dot(p, expand(v), preferred_element_type=F32).astype(BF16)
        loop(rows // 2, tokens, fn, unroll=4)

    def out_proj(l):
        def fn(r):
            d = jnp.dot(u[pl.ds(r, MB), :], weight(4, 1), preferred_element_type=F32) + bias(l, 9)
            x = out_ref[pl.ds(r, MB), :].astype(F32)
            out_ref[pl.ds(r, MB), :] = (x + wide(2, r, MB) * d).astype(BF16)
        loop(rows, MB, fn)

    def fc1(l, g):
        def fn(r):
            d = jnp.dot(u[pl.ds(r, MB), :], weight(7 + g // 2, g % 2), preferred_element_type=F32) + bias(l, 10 + g)
            h[pl.ds(r, MB), :] = jax.nn.gelu(d, approximate=True).astype(BF16)
        loop(rows, MB, fn)

    def fc2(l, g):
        def fn(r):
            d = jnp.dot(h[pl.ds(r, MB), :], f2[g * hidden:(g + 1) * hidden, :], preferred_element_type=F32)
            if g > 0:
                d = acc[pl.ds(r, MB), :] + d
            if g < 3:
                acc[pl.ds(r, MB), :] = d
            else:
                x = out_ref[pl.ds(r, MB), :].astype(F32)
                out_ref[pl.ds(r, MB), :] = (x + wide(5, r, MB) * (d + bias(l, 14))).astype(BF16)
        loop(rows, MB, fn)

    plan = {
        (0, 0): [("prev", lambda l: fc1(l, 2))], (0, 1): [("", lambda l: modulation(l, 0))],
        (0, 2): [("prev", lambda l: fc2(l, 2))],
        (1, 0): [("prev", lambda l: fc1(l, 3))], (1, 1): [("", lambda l: modulation(l, 1))],
        (1, 2): [("prev", lambda l: fc2(l, 3))],
        (2, 1): [("", lambda l: modulation(l, 2))], (2, 2): [("", lambda l: norm_to_u(0, 1))],
        (3, 1): [("", lambda l: project(l, 0, 3, 0))], (3, 2): [("", lambda l: project(l, 1, 3, 1))],
        (4, 0): [("", lambda l: scores(0))], (4, 1): [("", lambda l: project(l, 2, 4, 0))],
        (4, 2): [("", lambda l: scores(1))],
        (5, 0): [("", lambda l: softmax())], (5, 1): [("", lambda l: values(0))], (5, 2): [("", lambda l: values(1))],
        (6, 0): [("", lambda l: out_proj(l))], (6, 1): [("", lambda l: norm_to_u(3, 4))],
        (7, 1): [("", lambda l: fc1(l, 0))], (7, 2): [("", lambda l: fc2(l, 0))],
        (8, 1): [("", lambda l: fc1(l, 1))], (8, 2): [("", lambda l: fc2(l, 1))],
    }

    def compute(c, part):
        layer, kk = c // pairs, c % pairs
        for (pair, when), tasks in plan.items():
            if when != part:
                continue
            for mark, task in tasks:
                if mark:
                    cond = jnp.logical_and(kk == pair, c >= pairs)
                    cl = layer - 1
                else:
                    cond = jnp.logical_and(kk == pair, jnp.logical_and(c >= 0, c < n))
                    cl = layer

                @pl.when(cond)
                def _(task=task, cl=cl):
                    task(cl)

    def within(k, fn):
        @pl.when(jnp.logical_and(k >= 0, k < n))
        def _():
            fn(k)

    lag = 4

    def plain(c):
        kk = c % pairs
        return jnp.logical_and(jnp.logical_and(c >= 0, c < n), jnp.logical_or(kk < first, kk >= last))

    def step(t, carry):
        c = t - lag
        within(t, start_pair)
        within(t - 2, gat.e3)
        within(c, gat.e6)

        @pl.when(plain(c))
        def _():
            load_pair(c).start()

        @pl.when(jnp.logical_and(c % pairs == last - 1, jnp.logical_and(c >= 0, c < n)))
        def _():
            load_f2(c).start()

        @pl.when(t == 0)
        def _():
            fill_mask()
            v = cond_ref[...].astype(F32)
            act[...] = jax.nn.silu(v).astype(BF16)
            out_ref[...] = x_ref[...]

        compute(c, 0)
        within(t - 1, gat.e2)
        within(t - 3, gat.e5)

        @pl.when(plain(c))
        def _():
            load_pair(c).wait()

        @pl.when(jnp.logical_and(c % pairs == last, jnp.logical_and(c >= 0, c < n)))
        def _():
            load_f2(c).wait()

        compute(c, 1)
        within(t, gat.e1)
        within(t - 2, gat.e4)
        compute(c, 2)
        return carry

    lax.fori_loop(0, n + lag + 2, step, 0)


def run_blocks(side, cond, x, bias, ada, qkvw, proj, fc1, fc2, tokens):
    rows, hidden = x.shape
    layers = ada.shape[0]
    n = layers * 9
    vm = pl.BlockSpec(memory_space=pltpu.VMEM)
    hk = NUM_HEADS * tokens
    dma = pltpu.SemaphoreType.DMA
    out, _ = pl.pallas_call(
        functools.partial(blocks_kernel, side, layers, tokens),
        out_shape=(jax.ShapeDtypeStruct((rows, hidden), BF16), jax.ShapeDtypeStruct((2 * n * hidden, hidden), BF16)),
        in_specs=[vm] * 8,
        out_specs=(vm, pl.BlockSpec(memory_space=pl.ANY)),
        scratch_shapes=[
            pltpu.VMEM(cond.shape, BF16), pltpu.VMEM((6,) + cond.shape, F32), pltpu.VMEM((rows, hidden), BF16),
            pltpu.VMEM((3, rows, hidden), BF16), pltpu.VMEM((rows, hidden), BF16), pltpu.VMEM((rows, hidden), F32),
            pltpu.VMEM((3, 2 * hidden, hidden), BF16), pltpu.VMEM((4 * hidden, hidden), BF16),
            pltpu.VMEM((hk, hidden), BF16), pltpu.VMEM((rows, hk), F32), dma((3,)), dma((1,)),
            dma((n, 15)), dma((n, 15)), dma((n, 16)), dma((n, 16)), dma((n,)),
        ],
        compiler_params=pltpu.CompilerParams(collective_id=0, has_side_effects=True, vmem_limit_bytes=67043328),
        name="dit_blocks",
    )(cond, x, bias, ada, qkvw, proj, fc1, fc2)
    return out


def solution(mesh):
    n_dev = mesh.shape["fsdp"]
    side = math.isqrt(n_dev // 2)
    batch_spec = P(("dp", "fsdp"), None, None)
    cond_spec = P(("dp", "fsdp"), None)
    shard_spec = P(None, "fsdp", None)
    bias_spec = P(None, None)

    def local_run(latents, cond_emb, w_ada, b_ada, w_qkv, b_qkv, w_proj, b_proj, w_fc1, b_fc1, w_fc2, b_fc2):
        samples, tokens, hidden = latents.shape
        layers = w_ada.shape[0]
        core = lax.axis_index("fsdp") % 2
        swap = [(i, i + 1 - 2 * (i % 2)) for i in range(n_dev)]

        def both(w):
            other = lax.ppermute(w, "fsdp", swap)
            return jnp.concatenate([jnp.where(core == 0, w, other), jnp.where(core == 0, other, w)], axis=1)

        bias = jnp.concatenate([b.astype(F32).reshape(layers, -1, hidden) for b in (b_ada, b_qkv, b_proj, b_fc1, b_fc2)],
                               axis=1)
        out = run_blocks(side, cond_emb, latents.reshape(samples * tokens, hidden), bias, both(w_ada), both(w_qkv),
                         both(w_proj), both(w_fc1), w_fc2, tokens)
        return out.reshape(latents.shape)

    in_specs = (batch_spec, cond_spec, shard_spec, bias_spec, shard_spec, bias_spec, shard_spec, bias_spec, shard_spec,
                bias_spec, shard_spec, bias_spec)
    return jax.shard_map(local_run, mesh=mesh, in_specs=in_specs, out_specs=batch_spec, check_vma=False)
```

time: 765 us -> 357 us (0.47)
  waiting for transfers between devices: 377 us -> 0.01 us
  Pallas kernels: 0 us -> 336 us
  matrix products: 173 us -> 0 us
  local copies, waits for them, and re-layouts: 110 us -> 8.27 us
  other arithmetic: 83.2 us -> 7.2 us
  between operations: 14.3 us -> 0.05 us
    all_gather x10 -> x0, waiting for transfers between devices: 374 us -> none  [gather_rows(): return lax.all_gather(shard, 'fsdp', axis=0, tiled=True)]
    pallas_call x0 -> x1, Pallas kernels: none -> 336 us  [run_blocks(): pl.pallas_call(functools.partial(blocks_kernel, side, layers, tokens), ou...]
    dot_general x13 -> x0, matrix products: 173 us -> none  [the longest x2 58.5 us: value_a9(): jnp.einsum('snf,fd->snd', hidden_act, full_fc2, preferred_element_type=jn...]
    reshape x6 -> x5, local copies, waits for them, and re-layouts: 71.7 us -> 3.67 us  [local_run(): b.astype(F32).reshape(layers, -1, hidden)]
    sub x2 -> x0, other arithmetic: 66.6 us -> none  [value_a9(): attn_probs = jax.nn.softmax(scores, axis=-1).astype(jnp.bfloat16)]
    slice x7 -> x0, local copies, waits for them, and re-layouts: 25.5 us -> none  [the longest x2 14.9 us: value_a9(): qkv_rows[:, :, 2]]
    slice x2 -> x0, other arithmetic: 11 us -> none  [value_a9(): gate_m = mod_parts[:, 5]]
  transfers between devices with their start and end apart: 10 -> 4, of which waited for: 9 -> 0; matrix products, arithmetic and copies ran while one was open for 42% -> 3% of each run, Pallas kernels for 0% -> 0%
where the time goes in v1:
time: 357 us; the launch traced here: 355 us
  Pallas kernels  336 us (94%)
  local copies, waits for them, and re-layouts  8.27 us (2%)
  other arithmetic  7.2 us (2%)
    pallas_call x1, Pallas kernels, run_blocks(): pl.pallas_call(functools.partial(blocks_kernel, side, layers, tokens), ou...  336 us
  transfers between devices with their start and end apart: 4, of which 0 were waited for; matrix products, arithmetic and copies ran while one was open for 3% of the time, Pallas kernels for 0%

profile of v1, /device:TPU:97, one launch (start us, length us, event | category | flops | bytes accessed | tf_op | source)
XLA Modules:
  0.0 354.6 jit_solution(4778658581835856650)
XLA Ops:
  0.0 0.0 copy-start.2
  0.0 1.0 copy.50
  1.0 2.1 collective-permute-start.2
  3.1 0.1 collective-permute-start.1
  3.3 0.4 collective-permute-start.3
  3.6 0.1 collective-permute-start
  3.8 0.7 copy.39
  4.5 0.7 copy.40
  5.2 0.7 reshape.28
  5.9 0.7 reshape.30
  6.6 0.8 reshape.27
  7.4 0.2 concatenate.17
  7.7 0.7 concatenate.18.bias_ref
  8.3 0.0 collective-permute-done.2
  8.4 1.0 broadcast_select_fusion.7
  9.3 0.8 pad_maximum_fusion.3.proj_ref
  10.1 0.0 copy-start.1
  10.1 0.0 collective-permute-done.1
  10.2 0.0 copy-done.2
  10.2 0.3 broadcast_select_fusion.5
  10.4 1.1 pad_maximum_fusion.2.qkvw_ref
  11.5 0.0 collective-permute-done.3
  11.5 0.0 copy-done.1
  11.6 0.2 broadcast_select_fusion.3
  11.8 0.0 copy-start
  11.8 1.3 pad_maximum_fusion.1.fc1_ref
  13.0 0.0 collective-permute-done
  13.0 0.1 copy-done
  13.1 0.3 broadcast_select_fusion.1
  13.4 1.6 pad_maximum_fusion.ada_ref
  15.0 336.3 %dit_blocks.1 = (bf16[1024,1152]{1,0:T(8,128)(2,1)}, bf16[41472,1152]{1,0:T(8,128)(2,1)}) custom-call(bf16[64,1152]{1,0:T(8,128)(2,1)} %cond_ref.1, bf16[1024,1152]{1,0:T(8,128)(2,1)} %bitcast.5, f32[2,15,1152]{2,1,0:T(8,128)} %concatenate.18.bias_ref, bf16[2,72,6912]{2,1,0:T(8,128)(2,1)} %pad_maximum_fusion.ada_ref, ...), custom_call_target="tpu_custom_call" | custom-call | tf_op jit(solution)/shard_map/dit_blocks/pallas_call | solution.py:379
  351.4 3.3 copy.71
Async XLA Ops:
  0.0 10.2 %copy-start.2 = (bf16[2,36,3456]{2,0,1:T(2,128)(2,1)S(1)}, bf16[2,36,3456]{2,0,1:T(2,128)(2,1)}, u32[]{:S(2)}) copy-start(bf16[2,36,3456]{2,0,1:T(2,128)(2,1)} %param.16) | copy-start | bytes 1492996
  1.0 7.4 %collective-permute-start.2 = (bf16[2,36,1152]{2,1,0:T(8,128)(2,1)S(1)}, bf16[2,36,1152]{2,1,0:T(8,128)(2,1)S(1)}, u32[]{:S(2)}, u32[]{:S(2)}) collective-permute-start(bf16[2,36,1152]{2,1,0:T(8,128)(2,1)S(1)} %copy.50), channel_id=1, source_target_pairs={{0,1},{1,0},{2,3},{3,2},{4,5},{5,4},{6,7},{7,6},{8,9},{9,8},{10,11... | collective-permute-start | bytes 497672 | tf_op jit(solution)/shard_map/ppermute | solution.py:412
  3.1 7.0 %collective-permute-start.1 = (bf16[2,36,3456]{2,0,1:T(2,128)(2,1)}, bf16[2,36,3456]{2,0,1:T(2,128)(2,1)S(1)}, u32[]{:S(2)}, u32[]{:S(2)}) collective-permute-start(bf16[2,36,3456]{2,0,1:T(2,128)(2,1)} %param.16), channel_id=1, source_target_pairs={{0,1},{1,0},{2,3},{3,2},{4,5},{5,4},{6,7},{7,6},{8,9},{9,8},{10,11... | collective-permute-start | bytes 1493000 | tf_op jit(solution)/shard_map/ppermute | solution.py:412
  3.3 8.3 %collective-permute-start.3 = (bf16[2,36,4608]{2,0,1:T(2,128)(2,1)}, bf16[2,36,4608]{2,0,1:T(2,128)(2,1)S(1)}, u32[]{:S(2)}, u32[]{:S(2)}) collective-permute-start(bf16[2,36,4608]{2,0,1:T(2,128)(2,1)} %param.20), channel_id=1, source_target_pairs={{0,1},{1,0},{2,3},{3,2},{4,5},{5,4},{6,7},{7,6},{8,9},{9,8},{10,11... | collective-permute-start | bytes 1990664 | tf_op jit(solution)/shard_map/ppermute | solution.py:412
  3.6 9.4 %collective-permute-start = (bf16[2,36,6912]{2,0,1:T(2,128)(2,1)}, bf16[2,36,6912]{2,0,1:T(2,128)(2,1)S(1)}, u32[]{:S(2)}, u32[]{:S(2)}) collective-permute-start(bf16[2,36,6912]{2,0,1:T(2,128)(2,1)} %param.14), channel_id=1, source_target_pairs={{0,1},{1,0},{2,3},{3,2},{4,5},{5,4},{6,7},{7,6},{8,9},{9,8},{10,11... | collective-permute-start | bytes 2985992 | tf_op jit(solution)/shard_map/ppermute | solution.py:412
  10.1 1.4 copy-start.1
  11.8 1.4 copy-start

commit v2 on v1

--- a/solution.py
+++ b/solution.py
@@ -35,6 +35,9 @@
     def dev(self, f, g):
         return {"fsdp": self.chip(self.core, f, g) * 2 + self.core}
 
+    def at(self, chip, core):
+        return {"fsdp": chip * 2 + core}
+
     def partner(self):
         return {"fsdp": self.chip(self.core, 0, 0) * 2 + 1 - self.core}
 
@@ -42,7 +45,7 @@
         pairs, first, last = self.kinds
         chip = self.chip(core, f, g)
         layer, kk = k // pairs, k % pairs
-        own_order = kk // first - kk // last
+        own_order = kk // first - 2 * (kk // last)
         count = last - first
         plain = (2 * kk + core) * self.unit + chip * self.rows
         ordered = 2 * first * self.unit + ((chip * 2 + core) * count + kk - first) * self.rows
@@ -59,7 +62,9 @@
 
     def barrier(self):
         sem = pltpu.get_barrier_semaphore()
-        peers = [self.dev(1, 0), self.dev(-1, 0), self.dev(0, 1), self.dev(0, -1), self.partner()]
+        peers = [self.partner()]
+        for core in (0, 1):
+            peers += [self.at(self.chip(way, o, 0), core) for way in (0, 1) for o in range(1, self.side)]
         for p in peers:
             pl.semaphore_signal(sem, inc=1, device_id=p, device_id_type=MESH)
         pl.semaphore_wait(sem, len(peers))
@@ -139,20 +144,183 @@
         pltpu.make_async_copy(own, own, self.lsem.at[k]).wait()
 
 
+class Modulation:
+    def __init__(self, gat, layers, ada, bias, cond, land, conds, act, made, mods, csem, crecv, asem, arecv, gsem, grecv,
+                 msem, mrecv):
+        self.gat, self.layers, self.ada, self.bias, self.cond = gat, layers, ada, bias, cond
+        self.land, self.conds, self.act, self.made, self.mods = land, conds, act, made, mods
+        self.csem, self.crecv, self.asem, self.arecv = csem, crecv, asem, arecv
+        self.gsem, self.grecv, self.msem, self.mrecv = gsem, grecv, msem, mrecv
+        self.side, self.core = gat.side, gat.core
+        self.f = gat.x * (1 - gat.core) + gat.y * gat.core
+        self.count = 3 * layers
+        self.samples = cond.shape[0]
+
+    def remote(self, src, dst, send, recv, to):
+        return pltpu.make_async_remote_copy(src_ref=src, dst_ref=dst, send_sem=send, recv_sem=recv, device_id=to,
+                                            device_id_type=MESH)
+
+    def cond_slot(self, i):
+        return self.conds.at[pl.ds(pl.multiple_of(i * self.samples, 16), self.samples), :]
+
+    def rows_of(self, slot, f, g):
+        row = slot * self.gat.unit + self.gat.chip(self.core, f, g) * self.gat.rows
+        return self.land.at[pl.ds(pl.multiple_of(row, 8), self.gat.rows), :]
+
+    def own(self, j):
+        col = (2 * (j % 3) + self.core) * self.gat.unit
+        return self.ada.at[j // 3, :, pl.ds(pl.multiple_of(col, 128), self.gat.unit)]
+
+    def owned(self, fn):
+        for slot in range(-(-self.count // self.side)):
+            @pl.when(self.f + slot * self.side < self.count)
+            def _(slot=slot):
+                fn(slot)
+
+    def a0(self):
+        gat, side = self.gat, self.side
+        pltpu.make_async_copy(self.cond, self.cond_slot(self.core), self.csem.at[0]).start()
+        self.remote(self.cond, self.cond_slot(self.core), self.csem.at[1], self.crecv.at[self.core], gat.partner()).start()
+        for way in (0, 1):
+            for o in range(1, side):
+                i = (side - o) * 2 + self.core
+                self.remote(self.cond, self.cond_slot(i), self.csem.at[2 + way * side + o], self.crecv.at[i],
+                            gat.at(gat.chip(way, o, 0), way)).start()
+        for j in range(self.count):
+            o = (j % side - self.f + side) % side
+            dst = self.rows_of(j // side, 0, 0)
+
+            @pl.when(o == 0)
+            def _(j=j, dst=dst):
+                pltpu.make_async_copy(self.own(j), dst, self.asem.at[j]).start()
+
+            @pl.when(o != 0)
+            def _(j=j, o=o, dst=dst):
+                self.remote(self.own(j), dst, self.asem.at[j], self.arecv.at[j // side, (side - o) % side],
+                            gat.dev(o, 0)).start()
+
+    def ring(self, slot, r, w, f, g, to):
+        p = self.rows_of(slot, f, g)
+        i = 3 * r + w
+        return self.remote(p, p, self.gsem.at[slot, i], self.grecv.at[slot, i], to)
+
+    def a1(self):
+        gat = self.gat
+
+        def fn(slot):
+            for r in range(self.side):
+                p = self.rows_of(slot, r, 0)
+                if r == 0:
+                    pltpu.make_async_copy(p, p, self.asem.at[self.f + slot * self.side]).wait()
+                else:
+                    self.remote(p, p, self.asem.at[0], self.arecv.at[slot, r], gat.partner()).wait_recv()
+                self.ring(slot, r, 0, r, 0, gat.dev(0, 1)).start()
+                self.ring(slot, r, 1, r, 0, gat.dev(0, -1)).start()
+        self.owned(fn)
+
+    def a2(self):
+        def fn(slot):
+            for r in range(self.side):
+                self.ring(slot, r, 0, r, -1, self.gat.partner()).wait_recv()
+                self.ring(slot, r, 1, r, 1, self.gat.partner()).wait_recv()
+                d = 1 - 2 * (r % 2)
+                self.ring(slot, r, 2, r, -d, self.gat.dev(0, d)).start()
+        self.owned(fn)
+
+    def made_part(self, slot, i):
+        return self.made.at[slot, pl.ds(pl.multiple_of(i * self.samples, 16), self.samples), :]
+
+    def a3(self):
+        gat, side, unit = self.gat, self.side, self.gat.unit
+        people = 2 * side * self.samples
+        pltpu.make_async_copy(self.cond, self.cond_slot(self.core), self.csem.at[0]).wait()
+        for i in range(2 * side):
+            @pl.when(self.core != i)
+            def _(i=i):
+                self.remote(self.cond, self.cond_slot(i), self.csem.at[1], self.crecv.at[i], gat.partner()).wait_recv()
+        blk = people // 4
+
+        def silu(b, carry):
+            r = pl.multiple_of(b * blk, blk)
+            self.act[pl.ds(r, blk), :] = jax.nn.silu(self.conds[pl.ds(r, blk), :].astype(F32)).astype(BF16)
+            return carry
+        lax.fori_loop(0, 4, silu, 0)
+
+        def fn(slot):
+            for r in range(side):
+                self.ring(slot, r, 2, r, 2, gat.partner()).wait_recv()
+            j = self.f + slot * side
+            layer, i = j // 3, 2 * (j % 3) + self.core
+            row = self.bias[layer, pl.ds(i, 1), :]
+
+            def mul(b, carry):
+                r = pl.multiple_of(b * blk, blk)
+                d = jnp.dot(self.act[pl.ds(r, blk), :], self.land[slot * unit:(slot + 1) * unit, :],
+                            preferred_element_type=F32)
+                self.made[slot, pl.ds(r, blk), :] = (d + row).astype(BF16)
+                return carry
+            lax.fori_loop(0, 4, mul, 0)
+            dst = self.mods.at[layer * 6 + i]
+            sem = self.mrecv.at[layer * 6 + i]
+            for o in range(side):
+                for core in (0, 1):
+                    q = 2 * o + core
+                    src = self.made_part(slot, q)
+                    if o:
+                        self.remote(src, dst, self.msem.at[slot, q], sem, gat.at(gat.chip(self.core, o, 0), core)).start()
+                    else:
+                        @pl.when(self.core == core)
+                        def _(src=src):
+                            pltpu.make_async_copy(src, dst, sem).start()
+
+                        @pl.when(self.core != core)
+                        def _(src=src, q=q):
+                            self.remote(src, dst, self.msem.at[slot, q], sem, gat.partner()).start()
+        self.owned(fn)
+
+    def a4(self):
+        gat, side = self.gat, self.side
+        for i in range(2 * self.count):
+            m = self.mods.at[i]
+            pltpu.make_async_copy(m, m, self.mrecv.at[i]).wait()
+        c = self.cond
+        self.remote(c, c, self.csem.at[1], self.crecv.at[0], gat.partner()).wait_send()
+        for way in (0, 1):
+            for o in range(1, side):
+                self.remote(c, c, self.csem.at[2 + way * side + o], self.crecv.at[0], gat.partner()).wait_send()
+        for j in range(self.count):
+            @pl.when((j % side - self.f + side) % side != 0)
+            def _(j=j):
+                p = self.own(j)
+                self.remote(p, p, self.asem.at[j], self.arecv.at[0, 0], gat.partner()).wait_send()
+
+        def fn(slot):
+            for r in range(side):
+                for w in range(3):
+                    self.ring(slot, r, w, r, 0, gat.partner()).wait_send()
+            for q in range(2 * side):
+                @pl.when(self.core != q)
+                def _(q=q):
+                    p = self.made_part(slot, q)
+                    self.remote(p, p, self.msem.at[slot, q], self.mrecv.at[0], gat.partner()).wait_send()
+        self.owned(fn)
+
+
 def normed(v):
     c = v - jnp.mean(v, axis=-1, keepdims=True)
     return c * lax.rsqrt(jnp.mean(c * c, axis=-1, keepdims=True) + LN_EPS)
 
 
 def blocks_kernel(side, layers, tokens, cond_ref, x_ref, bias_ref, ada_ref, qkvw_ref, proj_ref, fc1_ref, fc2_ref, out_ref,
-                  gw, act, mods, u, qkv, h, acc, wslot, f2, mask, s_ref, wsem, f2sem, *sems):
+                  gw, mods, u, qkv, h, acc, wslot, f2, mask, seg, s_ref, wsem, f2sem, *sems):
     rows, hidden = out_ref.shape
     heads, dim = NUM_HEADS, hidden // NUM_HEADS
     hk = heads * tokens
-    pairs, first, last = 9, 5, 7
+    pairs, first, last = 6, 2, 4
     n = layers * pairs
-    gat = Gather(side, gw, hidden, (pairs, first, last), *sems)
+    gat = Gather(side, gw, hidden, (pairs, first, last), *sems[:5])
     core, piece_rows = gat.core, gat.rows
+    mod = Modulation(gat, layers, ada_ref, bias_ref, cond_ref, wslot.at[2], u, h, qkv, mods, *sems[5:])
 
     gat.barrier()
 
@@ -166,12 +334,11 @@
                              pl.ds(pl.multiple_of(col * hidden, 128), hidden)]
                 gat.e0(k, own)
 
-        send(kk < 3, ada_ref, 2 * kk + core)
-        send(kk == 3, qkvw_ref, core)
-        send(jnp.logical_and(kk == 4, core == 0), qkvw_ref, 2)
-        send(jnp.logical_and(kk == 4, core == 1), proj_ref, 0)
-        send(jnp.logical_and(kk >= 5, kk < 7), fc2_ref, 0, (kk - 5) * piece_rows)
-        send(kk >= 7, fc1_ref, 2 * (kk - 7) + core)
+        send(kk == 0, qkvw_ref, core)
+        send(jnp.logical_and(kk == 1, core == 0), qkvw_ref, 2)
+        send(jnp.logical_and(kk == 1, core == 1), proj_ref, 0)
+        send(jnp.logical_and(kk >= first, kk < last), fc2_ref, 0, (kk - first) * piece_rows)
+        send(kk >= last, fc1_ref, 2 * (kk - last) + core)
 
     def load_pair(c):
         return pltpu.make_async_copy(gw.at[pl.ds(pl.multiple_of(2 * c * hidden, 8), 2 * hidden), :],
@@ -186,6 +353,8 @@
         row = lax.broadcasted_iota(jnp.int32, (hk, hidden), 0)
         lo = (row // tokens) * dim
         mask[...] = jnp.where(jnp.logical_and(lane >= lo, lane < lo + dim), 1.0, 0.0).astype(BF16)
+        head = [lax.broadcasted_iota(jnp.int32, (hk, hk), d) // tokens for d in (0, 1)]
+        seg[...] = jnp.where(head[0] == head[1], 1.0, 0.0).astype(BF16)
 
     def loop(size, step, fn, unroll=1):
         def it(i, carry):
@@ -193,8 +362,8 @@
             return carry
         lax.fori_loop(0, size // step, it, 0, unroll=unroll)
 
-    def wide(j, r, size):
-        v = mods[j, pl.ds(pl.multiple_of(r // tokens, 8), size // tokens), :]
+    def wide(l, j, r, size):
+        v = mods[6 * l + j, pl.ds(pl.multiple_of(r // tokens, 16), size // tokens), :].astype(F32)
         return jnp.broadcast_to(v[:, None, :], (size // tokens, tokens, hidden)).reshape(size, hidden)
 
     def weight(kk, half):
@@ -203,18 +372,12 @@
     def bias(l, i):
         return bias_ref[l, i:i + 1, :]
 
-    def modulation(l, kk):
-        for half in (0, 1):
-            j = 2 * kk + half
-            d = jnp.dot(act[...], weight(kk, half), preferred_element_type=F32)
-            mods[j] = (d + bias(l, j)).astype(BF16).astype(F32)
-
-    LB, MB = 128, 256
-
-    def norm_to_u(shift, scale):
+    LB, MB = 256, 256
+
+    def norm_to_u(l, shift, scale):
         def fn(r):
             v = normed(out_ref[pl.ds(r, LB), :].astype(F32))
-            u[pl.ds(r, LB), :] = (v * (1.0 + wide(scale, r, LB)) + wide(shift, r, LB)).astype(BF16)
+            u[pl.ds(r, LB), :] = (v * (1.0 + wide(l, scale, r, LB)) + wide(l, shift, r, LB)).astype(BF16)
         loop(rows, LB, fn)
 
     def project(l, j, kk, half):
@@ -236,19 +399,21 @@
         loop(rows // 2, tokens, fn, unroll=4)
 
     def softmax():
-        blk = 64
-
-        def segment(v, op, lane_id):
-            for sh in (8, 4, 2, 1):
-                up, down = pltpu.roll(v, hk - sh, 1), pltpu.roll(v, sh, 1)
-                v = op(v, jnp.where((lane_id // sh) % 2 == 0, up, down))
-            return v
-
-        def fn(r):
-            lane_id = lax.broadcasted_iota(jnp.int32, (blk, hk), 1)
-            s = s_ref[pl.ds(r, blk), :] * (dim ** -0.5)
-            e = jnp.exp(s - segment(s, jnp.maximum, lane_id))
-            s_ref[pl.ds(r, blk), :] = e / segment(e, jnp.add, lane_id)
+        blk = 256
+
+        def fn(r):
+            even = [(lax.broadcasted_iota(jnp.int32, (blk, hk), 1) // sh) % 2 == 0 for sh in (8, 4, 2, 1)]
+            v = s_ref[pl.ds(r, blk), :] * (dim ** -0.5)
+            top = v
+            for sh, cond in zip((8, 4, 2, 1), even):
+                top = jnp.maximum(top, jnp.where(cond, pltpu.roll(top, hk - sh, 1), pltpu.roll(top, sh, 1)))
+            e = jnp.exp(v - top)
+            total, rest = 0.0, e
+            for _ in range(3):
+                part = rest.astype(BF16)
+                total = total + jnp.dot(part, seg[...], preferred_element_type=F32)
+                rest = rest - part.astype(F32)
+            s_ref[pl.ds(r, blk), :] = e / total
         loop(rows, blk, fn)
 
     def values(half):
@@ -261,14 +426,14 @@
 
     def out_proj(l):
         def fn(r):
-            d = jnp.dot(u[pl.ds(r, MB), :], weight(4, 1), preferred_element_type=F32) + bias(l, 9)
+            d = jnp.dot(u[pl.ds(r, MB), :], weight(1, 1), preferred_element_type=F32) + bias(l, 9)
             x = out_ref[pl.ds(r, MB), :].astype(F32)
-            out_ref[pl.ds(r, MB), :] = (x + wide(2, r, MB) * d).astype(BF16)
+            out_ref[pl.ds(r, MB), :] = (x + wide(l, 2, r, MB) * d).astype(BF16)
         loop(rows, MB, fn)
 
     def fc1(l, g):
         def fn(r):
-            d = jnp.dot(u[pl.ds(r, MB), :], weight(7 + g // 2, g % 2), preferred_element_type=F32) + bias(l, 10 + g)
+            d = jnp.dot(u[pl.ds(r, MB), :], weight(last + g // 2, g % 2), preferred_element_type=F32) + bias(l, 10 + g)
             h[pl.ds(r, MB), :] = jax.nn.gelu(d, approximate=True).astype(BF16)
         loop(rows, MB, fn)
 
@@ -281,22 +446,21 @@
                 acc[pl.ds(r, MB), :] = d
             else:
                 x = out_ref[pl.ds(r, MB), :].astype(F32)
-                out_ref[pl.ds(r, MB), :] = (x + wide(5, r, MB) * (d + bias(l, 14))).astype(BF16)
+                out_ref[pl.ds(r, MB), :] = (x + wide(l, 5, r, MB) * (d + bias(l, 14))).astype(BF16)
         loop(rows, MB, fn)
 
     plan = {
-        (0, 0): [("prev", lambda l: fc1(l, 2))], (0, 1): [("", lambda l: modulation(l, 0))],
-        (0, 2): [("prev", lambda l: fc2(l, 2))],
-        (1, 0): [("prev", lambda l: fc1(l, 3))], (1, 1): [("", lambda l: modulation(l, 1))],
-        (1, 2): [("prev", lambda l: fc2(l, 3))],
-        (2, 1): [("", lambda l: modulation(l, 2))], (2, 2): [("", lambda l: norm_to_u(0, 1))],
-        (3, 1): [("", lambda l: project(l, 0, 3, 0))], (3, 2): [("", lambda l: project(l, 1, 3, 1))],
-        (4, 0): [("", lambda l: scores(0))], (4, 1): [("", lambda l: project(l, 2, 4, 0))],
-        (4, 2): [("", lambda l: scores(1))],
-        (5, 0): [("", lambda l: softmax())], (5, 1): [("", lambda l: values(0))], (5, 2): [("", lambda l: values(1))],
-        (6, 0): [("", lambda l: out_proj(l))], (6, 1): [("", lambda l: norm_to_u(3, 4))],
-        (7, 1): [("", lambda l: fc1(l, 0))], (7, 2): [("", lambda l: fc2(l, 0))],
-        (8, 1): [("", lambda l: fc1(l, 1))], (8, 2): [("", lambda l: fc2(l, 1))],
+        (0, 0): [("prev", lambda l: fc1(l, 3))],
+        (0, 1): [("prev", lambda l: fc2(l, 3)), ("later", lambda l: norm_to_u(l, 0, 1))],
+        (0, 2): [("", lambda l: project(l, 0, 0, 0))],
+        (1, 0): [("", lambda l: project(l, 1, 0, 1))], (1, 1): [("", lambda l: scores(0))],
+        (1, 2): [("", lambda l: scores(1))],
+        (2, 0): [("", lambda l: project(l, 2, 1, 0))], (2, 1): [("", lambda l: softmax())],
+        (2, 2): [("", lambda l: values(0))],
+        (3, 0): [("", lambda l: values(1))], (3, 1): [("", lambda l: out_proj(l))],
+        (3, 2): [("", lambda l: norm_to_u(l, 3, 4))],
+        (4, 0): [("", lambda l: fc1(l, 0))], (4, 1): [("", lambda l: fc2(l, 0))], (4, 2): [("", lambda l: fc1(l, 1))],
+        (5, 0): [("", lambda l: fc2(l, 1))], (5, 1): [("", lambda l: fc1(l, 2))], (5, 2): [("", lambda l: fc2(l, 2))],
     }
 
     def compute(c, part):
@@ -305,7 +469,10 @@
             if when != part:
                 continue
             for mark, task in tasks:
-                if mark:
+                if mark == "later":
+                    cond = jnp.logical_and(kk == pair, jnp.logical_and(c >= pairs, c < n))
+                    cl = layer
+                elif mark:
                     cond = jnp.logical_and(kk == pair, c >= pairs)
                     cl = layer - 1
                 else:
@@ -329,50 +496,75 @@
 
     def step(t, carry):
         c = t - lag
+
+        @pl.when(t == 0)
+        def _():
+            mod.a0()
+
         within(t, start_pair)
         within(t - 2, gat.e3)
-        within(c, gat.e6)
 
         @pl.when(plain(c))
         def _():
-            load_pair(c).start()
-
-        @pl.when(jnp.logical_and(c % pairs == last - 1, jnp.logical_and(c >= 0, c < n)))
-        def _():
-            load_f2(c).start()
+            load_pair(c).wait()
+
+        @pl.when(jnp.logical_and(c % pairs == last, jnp.logical_and(c >= 0, c < n)))
+        def _():
+            load_f2(c).wait()
+
+        @pl.when(t == 1)
+        def _():
+            mod.a2()
+
+        @pl.when(t == 3)
+        def _():
+            mod.a4()
 
         @pl.when(t == 0)
         def _():
             fill_mask()
-            v = cond_ref[...].astype(F32)
-            act[...] = jax.nn.silu(v).astype(BF16)
             out_ref[...] = x_ref[...]
 
         compute(c, 0)
         within(t - 1, gat.e2)
         within(t - 3, gat.e5)
 
-        @pl.when(plain(c))
-        def _():
-            load_pair(c).wait()
-
-        @pl.when(jnp.logical_and(c % pairs == last, jnp.logical_and(c >= 0, c < n)))
-        def _():
-            load_f2(c).wait()
+        @pl.when(t == 0)
+        def _():
+            mod.a1()
+
+        @pl.when(t == 3)
+        def _():
+            norm_to_u(0, 0, 1)
 
         compute(c, 1)
         within(t, gat.e1)
         within(t - 2, gat.e4)
+        within(t - 3, gat.e6)
+
+        @pl.when(plain(c + 1))
+        def _():
+            load_pair(c + 1).start()
+
+        @pl.when(jnp.logical_and((c + 1) % pairs == last - 1, jnp.logical_and(c + 1 >= 0, c + 1 < n)))
+        def _():
+            load_f2(c + 1).start()
+
+        @pl.when(t == 1)
+        def _():
+            mod.a3()
+
         compute(c, 2)
         return carry
 
-    lax.fori_loop(0, n + lag + 2, step, 0)
+    lax.fori_loop(0, n + lag + 1, step, 0)
 
 
 def run_blocks(side, cond, x, bias, ada, qkvw, proj, fc1, fc2, tokens):
     rows, hidden = x.shape
     layers = ada.shape[0]
-    n = layers * 9
+    n = layers * 6
+    slots = -(-3 * layers // side)
     vm = pl.BlockSpec(memory_space=pltpu.VMEM)
     hk = NUM_HEADS * tokens
     dma = pltpu.SemaphoreType.DMA
@@ -382,11 +574,13 @@
         in_specs=[vm] * 8,
         out_specs=(vm, pl.BlockSpec(memory_space=pl.ANY)),
         scratch_shapes=[
-            pltpu.VMEM(cond.shape, BF16), pltpu.VMEM((6,) + cond.shape, F32), pltpu.VMEM((rows, hidden), BF16),
+            pltpu.VMEM((6 * layers,) + cond.shape, BF16), pltpu.VMEM((rows, hidden), BF16),
             pltpu.VMEM((3, rows, hidden), BF16), pltpu.VMEM((rows, hidden), BF16), pltpu.VMEM((rows, hidden), F32),
             pltpu.VMEM((3, 2 * hidden, hidden), BF16), pltpu.VMEM((4 * hidden, hidden), BF16),
-            pltpu.VMEM((hk, hidden), BF16), pltpu.VMEM((rows, hk), F32), dma((3,)), dma((1,)),
+            pltpu.VMEM((hk, hidden), BF16), pltpu.VMEM((hk, hk), BF16), pltpu.VMEM((rows, hk), F32), dma((3,)), dma((1,)),
             dma((n, 15)), dma((n, 15)), dma((n, 16)), dma((n, 16)), dma((n,)),
+            dma((2 + 2 * side,)), dma((2 * side,)), dma((3 * layers,)), dma((slots, side)), dma((slots, 3 * side)),
+            dma((slots, 3 * side)), dma((slots, 2 * side)), dma((6 * layers,)),
         ],
         compiler_params=pltpu.CompilerParams(collective_id=0, has_side_effects=True, vmem_limit_bytes=67043328),
         name="dit_blocks",

time: 357 us -> 308 us (0.86)
  Pallas kernels: 336 us -> 289 us
    pallas_call x1, Pallas kernels: 336 us -> 289 us  [run_blocks(): pl.pallas_call(functools.partial(blocks_kernel, side, layers, tokens), ou...]
where the time goes in v2:
time: 308 us; the launch traced here: 307 us
  Pallas kernels  289 us (94%)
  local copies, waits for them, and re-layouts  8.27 us (3%)
  other arithmetic  7.22 us (2%)
    pallas_call x1, Pallas kernels, run_blocks(): pl.pallas_call(functools.partial(blocks_kernel, side, layers, tokens), ou...  289 us
  transfers between devices with their start and end apart: 4, of which 0 were waited for; matrix products, arithmetic and copies ran while one was open for 3% of the time, Pallas kernels for 0%

profile of v2, /device:TPU:97, one launch (start us, length us, event | category | flops | bytes accessed | tf_op | source)
XLA Modules:
  0.0 307.0 jit_solution(17266782039889209233)
XLA Ops:
  0.0 0.0 copy-start.2
  0.0 1.0 copy.50
  1.0 2.1 collective-permute-start.2
  3.1 0.1 collective-permute-start.1
  3.3 0.4 collective-permute-start.3
  3.6 0.1 collective-permute-start
  3.8 0.7 copy.39
  4.5 0.7 copy.40
  5.2 0.7 reshape.28
  5.9 0.7 reshape.30
  6.6 0.8 reshape.27
  7.4 0.2 concatenate.17
  7.7 0.7 concatenate.18.bias_ref
  8.4 0.0 collective-permute-done.2
  8.4 1.0 broadcast_select_fusion.7
  9.3 0.8 pad_maximum_fusion.3.proj_ref
  10.1 0.0 copy-start.1
  10.1 0.0 collective-permute-done.1
  10.1 0.0 copy-done.2
  10.1 0.3 broadcast_select_fusion.5
  10.4 1.2 pad_maximum_fusion.2.qkvw_ref
  11.6 0.0 collective-permute-done.3
  11.6 0.0 copy-done.1
  11.6 0.2 broadcast_select_fusion.3
  11.8 0.0 copy-start
  11.8 1.3 pad_maximum_fusion.1.fc1_ref
  13.0 0.0 collective-permute-done
  13.0 0.1 copy-done
  13.1 0.3 broadcast_select_fusion.1
  13.5 1.6 pad_maximum_fusion.ada_ref
  15.1 288.7 %dit_blocks.1 = (bf16[1024,1152]{1,0:T(8,128)(2,1)}, bf16[27648,1152]{1,0:T(8,128)(2,1)}) custom-call(bf16[64,1152]{1,0:T(8,128)(2,1)} %cond_ref.1, bf16[1024,1152]{1,0:T(8,128)(2,1)} %bitcast.5, f32[2,15,1152]{2,1,0:T(8,128)} %concatenate.18.bias_ref, bf16[2,72,6912]{2,1,0:T(8,128)(2,1)} %pad_maximum_fusion.ada_ref, ...), custom_call_target="tpu_custom_call" | custom-call | tf_op jit(solution)/shard_map/dit_blocks/pallas_call | solution.py:571
  303.8 3.3 %copy.71 = bf16[64,16,1152]{2,1,0:T(8,128)(2,1)} copy(bf16[64,16,1152]{2,1,0:T(8,128)(2,1)} %bitcast.4) | data formatting | bytes 4718592
Async XLA Ops:
  0.0 10.1 %copy-start.2 = (bf16[2,36,3456]{2,0,1:T(2,128)(2,1)S(1)}, bf16[2,36,3456]{2,0,1:T(2,128)(2,1)}, u32[]{:S(2)}) copy-start(bf16[2,36,3456]{2,0,1:T(2,128)(2,1)} %param.16) | copy-start | bytes 1492996
  1.0 7.4 %collective-permute-start.2 = (bf16[2,36,1152]{2,1,0:T(8,128)(2,1)S(1)}, bf16[2,36,1152]{2,1,0:T(8,128)(2,1)S(1)}, u32[]{:S(2)}, u32[]{:S(2)}) collective-permute-start(bf16[2,36,1152]{2,1,0:T(8,128)(2,1)S(1)} %copy.50), channel_id=1, source_target_pairs={{0,1},{1,0},{2,3},{3,2},{4,5},{5,4},{6,7},{7,6},{8,9},{9,8},{10,11... | collective-permute-start | bytes 497672 | tf_op jit(solution)/shard_map/ppermute | solution.py:606
  3.1 7.0 %collective-permute-start.1 = (bf16[2,36,3456]{2,0,1:T(2,128)(2,1)}, bf16[2,36,3456]{2,0,1:T(2,128)(2,1)S(1)}, u32[]{:S(2)}, u32[]{:S(2)}) collective-permute-start(bf16[2,36,3456]{2,0,1:T(2,128)(2,1)} %param.16), channel_id=1, source_target_pairs={{0,1},{1,0},{2,3},{3,2},{4,5},{5,4},{6,7},{7,6},{8,9},{9,8},{10,11... | collective-permute-start | bytes 1493000 | tf_op jit(solution)/shard_map/ppermute | solution.py:606
  3.3 8.3 %collective-permute-start.3 = (bf16[2,36,4608]{2,0,1:T(2,128)(2,1)}, bf16[2,36,4608]{2,0,1:T(2,128)(2,1)S(1)}, u32[]{:S(2)}, u32[]{:S(2)}) collective-permute-start(bf16[2,36,4608]{2,0,1:T(2,128)(2,1)} %param.20), channel_id=1, source_target_pairs={{0,1},{1,0},{2,3},{3,2},{4,5},{5,4},{6,7},{7,6},{8,9},{9,8},{10,11... | collective-permute-start | bytes 1990664 | tf_op jit(solution)/shard_map/ppermute | solution.py:606
  3.6 9.4 %collective-permute-start = (bf16[2,36,6912]{2,0,1:T(2,128)(2,1)}, bf16[2,36,6912]{2,0,1:T(2,128)(2,1)S(1)}, u32[]{:S(2)}, u32[]{:S(2)}) collective-permute-start(bf16[2,36,6912]{2,0,1:T(2,128)(2,1)} %param.14), channel_id=1, source_target_pairs={{0,1},{1,0},{2,3},{3,2},{4,5},{5,4},{6,7},{7,6},{8,9},{9,8},{10,11... | collective-permute-start | bytes 2985992 | tf_op jit(solution)/shard_map/ppermute | solution.py:606
  10.1 1.4 copy-start.1
  11.8 1.4 copy-start
